TPU v7x, 32 devices: a whole 2x2x4 slice. The times are simulated.
32 devices in a mesh: region: 1, band: 32 (over z, y, x, core), tile: 1, sub: 1.
Axes of the slice: x: 2, y: 2, z: 4, core: 2. Of those that a mesh axis runs over, the one named last changes fastest.
Arguments:
- scenes: bfloat16 [60, 6, 1024, 128], P(('region', 'tile'), 'sub', 'band'), may hold values from -6 to 6
- clear_bits: int32 [2, 32, 256], P(('region', 'tile'), 'band'), may hold values from 0 to 1073741823
- footprint: int32 [60, 2], P(('region', 'tile')), may hold values from 0 to 31, as said below
- offsets: int32 [60, 2], P(('region', 'tile')), may hold values from 0 to 15
- acq_day: int32 [60], P(('region', 'tile')), may hold values from 0 to 364
Outputs:
- coefficients: float32 [8, 6, 128, 1024], P('region', 'sub', 'band', 'tile')
- monthly: float32 [12, 6, 128, 1024], P(('region', 'tile'), 'sub', 'band')
- annual: float32 [6, 128, 1024], P(('region', 'sub'), 'band', 'tile')
Inputs may be any that keep to these rules, and one draw needn't show every extreme that they name: `clear_bits`: bit j (j < 30) of word w at cell (b, a) is 1 when date 30 w + j is clear over columns 4 b to 4 b + 3 and rows 4 a to 4 a + 3. footprint[t, 0] <= footprint[t, 1]; date t's scene covers columns 4 * footprint[t, 0] to 4 * (footprint[t, 1] + 1) - 1. `offsets`: offsets in sixteenths of a pixel, along rows then columns.
All inputs are finite; a program needn't handle non-finite values.
Results may differ from a plain program's by a relative error of at most 0.005.
Values may be sent and summed in bfloat16 or wider, within the bound.
No kernel may reach another device: no remote copies, remote signals or barrier semaphores. Data moves between devices by JAX's collectives and lax.ppermute only.
A program may use at most 64 MiB of HBM per device.

v0:
```python
import functools

import jax
import jax.numpy as jnp
import numpy as np
from jax import lax
from jax.experimental import pallas as pl
from jax.experimental.pallas import tpu as pltpu
from jax.sharding import PartitionSpec as P

RIDGE = 1.0
STRIP = 4
TABLE = 8 * 26
PRODUCT = 8 * 84
EDGES = 64
FIT_VMEM = 60 * 1024 * 1024 - (8 << 20)


def shifted(value, axis, steps):
    count = lax.axis_size(axis)
    first, last = (max(0, -steps), min(count, count - steps))
    return lax.ppermute(value, axis, [(source, source + steps) for source in range(first, last)])


def extended(x, sides, width):
    for axis, dim in sides:
        devices, length = (lax.axis_size(axis), x.shape[dim])
        up = [(i, (i + 1) % devices) for i in range(devices - 1)]
        down = [(j, i) for i, j in up]
        last = lax.slice_in_dim(x, length - width, length, axis=dim)
        first = lax.slice_in_dim(x, 0, width, axis=dim)
        before = lax.ppermute(last, axis, up)
        after = lax.ppermute(first, axis, down)
        x = jnp.concatenate([before, x, after], axis=dim)
    return x


def design_tables(acq_day):
    day_phase = acq_day.astype(jnp.float32) / 365.0
    columns = [jnp.ones_like(day_phase), 2.0 * day_phase - 1.0]
    for harmonic in (1, 2, 3):
        turn_angle = 2.0 * jnp.pi * harmonic * day_phase
        columns = columns + [jnp.cos(turn_angle), jnp.sin(turn_angle)]
    harmonic_basis = jnp.stack(columns, axis=1)
    month_index = acq_day * 12 // 365
    onehot = (month_index[:, None] == jnp.arange(12, dtype=jnp.int32)[None, :]).astype(jnp.float32)
    products = jnp.stack(
        [
            harmonic_basis[:, row_term] * harmonic_basis[:, col_term]
            for row_term in range(8)
            for col_term in range(row_term + 1)
        ],
        axis=1,
    )
    return (
        jnp.concatenate([products, onehot], axis=1),
        jnp.concatenate([harmonic_basis, onehot], axis=1),
    )


def bilinear(padded, offsets):
    shift_row = (offsets[:, 0].astype(jnp.float32) / 16.0)[:, None, None, None]
    shift_col = (offsets[:, 1].astype(jnp.float32) / 16.0)[:, None, None, None]
    upper_rows = padded[:, :, :-1].astype(jnp.float32)
    lower_rows = padded[:, :, 1:].astype(jnp.float32)

    def across(source):
        right_cell = jnp.concatenate([source[..., 1:], jnp.zeros_like(source[..., :1])], axis=-1)
        return (1.0 - shift_col) * source + shift_col * right_cell

    return ((1.0 - shift_row) * across(upper_rows) + shift_row * across(lower_rows)).astype(
        jnp.bfloat16
    )


def clear_weight(cell_words, footprint, strip_width):
    date_count = footprint.shape[0]
    per_date = jnp.repeat(cell_words, 30, axis=0)
    bit_place = (jnp.arange(date_count, dtype=jnp.int32) % 30)[:, None, None]
    clear_flag = jnp.right_shift(per_date, bit_place) & 1
    pixel_flag = jnp.repeat(jnp.repeat(clear_flag, 4, axis=1), 4, axis=2)
    strip_index = jnp.arange(pixel_flag.shape[1], dtype=jnp.int32) // strip_width
    covered = (strip_index[None, :] >= footprint[:, 0:1]) & (
        strip_index[None, :] <= footprint[:, 1:2]
    )
    return pixel_flag.astype(jnp.float32) * covered[:, :, None].astype(jnp.float32)


def partial_sums(weight, values, common_table, banded_table):
    common = jnp.einsum("dxy,dk->kxy", weight, common_table, precision=lax.Precision.HIGHEST)
    weighted = values.astype(jnp.float32) * weight[:, None]
    banded = jnp.einsum("dsxy,dk->ksxy", weighted, banded_table, precision=lax.Precision.HIGHEST)
    return (common, banded)


def solve_normal(gram, rhs):
    pair_list = [(row_term, col_term) for row_term in range(8) for col_term in range(row_term + 1)]
    gram_entry = {}
    for position, term_pair in enumerate(pair_list):
        gram_entry[term_pair] = gram[position]
    factor = {}
    for col_term in range(8):
        pivot_value = gram_entry[col_term, col_term] + RIDGE
        for inner_term in range(col_term):
            pivot_value = pivot_value - factor[col_term, inner_term] * factor[col_term, inner_term]
        diag_root = jnp.sqrt(pivot_value)
        factor[col_term, col_term] = diag_root
        for row_term in range(col_term + 1, 8):
            running = gram_entry[row_term, col_term]
            for inner_term in range(col_term):
                running = running - factor[row_term, inner_term] * factor[col_term, inner_term]
            factor[row_term, col_term] = running / diag_root
    forward = []
    for row_term in range(8):
        running = rhs[row_term]
        for inner_term in range(row_term):
            running = running - factor[row_term, inner_term] * forward[inner_term]
        forward.append(running / factor[row_term, row_term])
    backward = [forward[0]] * 8
    for row_term in reversed(range(8)):
        running = forward[row_term]
        for inner_term in range(row_term + 1, 8):
            running = running - factor[inner_term, row_term] * backward[inner_term]
        backward[row_term] = running / factor[row_term, row_term]
    return jnp.stack(backward, axis=0)


def smooth_axis(padded_field, along):
    inner_size = padded_field.shape[along] - 2
    left_part = lax.slice_in_dim(padded_field, 0, inner_size, axis=along)
    centre_part = lax.slice_in_dim(padded_field, 1, inner_size + 1, axis=along)
    right_part = lax.slice_in_dim(padded_field, 2, inner_size + 2, axis=along)
    return 0.25 * left_part + 0.5 * centre_part + 0.25 * right_part


def split_dates(scenes, clear_bits, footprint, offsets, acq_day):
    date_count, band_count, row_local, col_count = scenes.shape
    strip_count = lax.axis_size("band")
    tile_count = lax.axis_size("tile")
    strip_width = col_count // strip_count
    row_count = row_local * strip_count
    common_table, banded_table = design_tables(acq_day)
    below = shifted(scenes[:, :, 0:1, :], "band", -1)
    resampled = bilinear(jnp.concatenate([scenes, below], axis=2), offsets)
    flipped = jnp.swapaxes(resampled, 2, 3)
    cell_words = lax.all_to_all(clear_bits, "band", split_axis=2, concat_axis=1, tiled=True)
    weight = clear_weight(cell_words, footprint, strip_width)
    common, banded = partial_sums(weight, flipped, common_table, banded_table)
    common, banded = (
        lax.all_to_all(common, "band", split_axis=1, concat_axis=2, tiled=True),
        lax.all_to_all(
            banded.reshape(-1, col_count, row_local),
            "band",
            split_axis=1,
            concat_axis=2,
            tiled=True,
        ),
    )
    banded = banded.reshape(20, band_count, strip_width, row_count)
    gram = common[:36]
    month_count = common[36:]
    rhs = banded[:8]
    month_sum = banded[8:]
    annual_sum = jnp.sum(month_sum, axis=0)
    annual_count = jnp.sum(month_count, axis=0)
    month_sum, month_count = (
        lax.psum_scatter(month_sum, "tile", scatter_dimension=0, tiled=True),
        lax.psum_scatter(month_count, "tile", scatter_dimension=0, tiled=True),
    )
    composite = month_sum / jnp.maximum(month_count, 1.0)[:, None]
    month_edged = extended(composite, (("band", 2),), 1)
    month_edged = jnp.pad(month_edged, ((0, 0), (0, 0), (0, 0), (1, 1)))
    monthly = smooth_axis(smooth_axis(month_edged, 3), 2)
    share = row_count // tile_count
    gram, rhs, annual_sum, annual_count = lax.psum((gram, rhs, annual_sum, annual_count), "tile")
    start = lax.axis_index("tile") * share
    gram = lax.dynamic_slice_in_dim(gram, start, share, 2)
    rhs = lax.dynamic_slice_in_dim(rhs, start, share, 3)
    annual_sum = lax.dynamic_slice_in_dim(annual_sum, start, share, 2)
    annual_count = lax.dynamic_slice_in_dim(annual_count, start, share, 1)
    coefficients = solve_normal(gram, rhs)
    yearly = annual_sum / jnp.maximum(annual_count, 1.0)
    year_edged = extended(yearly, (("band", 1), ("tile", 2)), 1)
    annual = smooth_axis(smooth_axis(year_edged, 2), 1)
    return (coefficients, monthly, annual)


def cdiv(a, b):
    return -(-a // b)


def lane_iota(shape, dim):
    return lax.broadcasted_iota(jnp.int32, shape, dim)


def fit_rows(day):
    phase = day / 365.0
    turn = 2.0 * jnp.pi * phase
    c, s = jnp.cos(turn), jnp.sin(turn)
    basis = [
        jnp.ones_like(phase),
        2.0 * phase - 1.0,
        c,
        s,
        2.0 * c * c - 1.0,
        2.0 * s * c,
        (4.0 * c * c - 3.0) * c,
        (3.0 - 4.0 * s * s) * s,
    ]
    months = [
        jnp.where((12.0 * day >= 365.0 * m) & (12.0 * day < 365.0 * (m + 1)), 1.0, 0.0) for m in range(12)
    ]
    return basis, months


def two_parts(entries):
    high = [row.astype(jnp.bfloat16).astype(jnp.float32) for row in entries]
    return high + [row - top for row, top in zip(entries, high)]


def fit_tables(day_ref, table_ref, edge_row, edge_lane):
    dates = day_ref.shape[1]
    width = 8 * dates
    day = jnp.broadcast_to(day_ref[...], (8, dates))
    digits = jnp.concatenate([day >> 4, day & 15], axis=0).astype(jnp.float32).astype(jnp.bfloat16)
    owner = lane_iota((dates, width), 1) // 8 == lane_iota((dates, width), 0)
    spread = jnp.dot(digits, jnp.where(owner, 1.0, 0.0).astype(jnp.bfloat16), preferred_element_type=jnp.float32)
    basis, months = fit_rows(16.0 * spread[:8] + spread[8:])
    products = [basis[i] * basis[j] for i in range(8) for j in range(i + 1)]
    diagonal = lane_iota((8, width), 1) % 8 == lane_iota((8, width), 0)
    short_basis, short_months = fit_rows(day.astype(jnp.float32))
    bottom = lane_iota((8, dates), 0) == 7
    for row0, lane0, keep, entries in (
        (0, 0, diagonal, two_parts(basis[1:]) + months),
        (TABLE, 0, diagonal, two_parts(products) + months),
        (edge_row, edge_lane, bottom, two_parts(short_basis[1:]) + short_months),
    ):
        for k in range(0, len(entries), 2):
            tile = jnp.concatenate([jnp.where(keep, row, 0.0) for row in entries[k : k + 2]], axis=0)
            table_ref[row0 + 8 * k : row0 + 8 * k + 16, lane0 : lane0 + keep.shape[1]] = tile.astype(jnp.bfloat16)


def own_words(words, first, bits_ref, b8):
    cells_here, cols = b8.shape[1:]
    strips, lanes = cols // STRIP, bits_ref.shape[1]
    blocks = bits_ref.shape[0] // strips // words
    block, within = first // lanes, lax.rem(first, lanes)
    lane = lane_iota((strips, lanes), 1)
    joined = jnp.zeros((strips, lanes), jnp.int32)
    for w in range(words):
        word = bits_ref[pl.ds(blocks * w + block, strips, stride=blocks * words), :]
        word = jnp.where(lane < cells_here, pltpu.roll(word, lax.rem(lanes - within, lanes), 1), 0)
        copies = word | pltpu.roll(word, cells_here, 1)
        copies = copies | pltpu.roll(copies, 2 * cells_here, 1)
        joined = joined | (pltpu.roll(copies, 4 * cells_here * w, 1) if w else copies)
    digits = lax.shift_right_logical(joined, 8 * (lane // cells_here % 4)) & 255
    mine = lane_iota((strips, cols), 1) // STRIP == lane_iota((strips, cols), 0)
    spread = lax.dot_general(
        digits.astype(jnp.float32).astype(jnp.bfloat16),
        jnp.where(mine, 1.0, 0.0).astype(jnp.bfloat16),
        (((0,), (0,)), ((), ())),
        preferred_element_type=jnp.float32,
    ).astype(jnp.int32)
    for w in range(words):
        parts = [spread[cells_here * (4 * w + k) : cells_here * (4 * w + k + 1)] << (8 * k) for k in range(4)]
        b8[w] = parts[0] | parts[1] | parts[2] | parts[3]


def solve_cells(g_ref, inv_ref):
    pairs = [(i, j) for i in range(8) for j in range(i + 1)]
    gram = {
        ij: g_ref[8 * n : 8 * n + 8] + g_ref[8 * (n + 36) : 8 * (n + 36) + 8] for n, ij in enumerate(pairs)
    }
    factor, root = {}, {}
    for j in range(8):
        root[j] = lax.rsqrt(gram[j, j] + RIDGE)
        for i in range(j + 1, 8):
            factor[i, j] = gram[i, j] * root[j]
        for k in range(j + 1, 8):
            for i in range(k, 8):
                gram[i, k] = gram[i, k] - factor[i, j] * factor[k, j]
    lower = {}
    for j in range(8):
        lower[j, j] = root[j]
        for i in range(j + 1, 8):
            running = factor[i, j] * lower[j, j]
            for k in range(j + 1, i):
                running = running + factor[i, k] * lower[k, j]
            lower[i, j] = -running * root[i]
    for n, (i, j) in enumerate(pairs):
        total = lower[i, i] * lower[i, j]
        for k in range(i + 1, 8):
            total = total + lower[k, i] * lower[k, j]
        inv_ref[n] = total
    counts = [g_ref[8 * (72 + m) : 8 * (72 + m) + 8] for m in range(12)]
    whole = counts[0]
    for m in range(1, 12):
        whole = whole + counts[m]
    for m in range(12):
        inv_ref[36 + m] = 1.0 / jnp.maximum(counts[m], 1.0)
    inv_ref[48] = 1.0 / jnp.maximum(whole, 1.0)


def resample_body(
    foot_far,
    offs_far,
    day_far,
    smooth_far,
    scene_far,
    x_far,
    table_far,
    foot_ref,
    offs_ref,
    day_ref,
    foot_rows,
    offs_rows,
    small_sem,
    scene,
    x_ref,
    table_ref,
    lines,
    in_sem,
    out_sem,
):
    f32, bf16 = jnp.float32, jnp.bfloat16
    dates, bands, rows, cols = scene.shape
    parts = rows // 8
    chunks = in_sem.shape[0] - 1
    chunk = dates // chunks
    table_rows, product_rows, width = TABLE, PRODUCT, table_ref.shape[1]
    smooth_row = table_rows + product_rows
    cover_row = smooth_row + 2 * cols

    def load(k):
        part = pl.ds(k * chunk, chunk)
        return pltpu.make_async_copy(scene_far.at[part], scene.at[part], in_sem.at[k])

    smooth = pltpu.make_async_copy(
        smooth_far, table_ref.at[pl.ds(smooth_row, 2 * cols), :], in_sem.at[chunks]
    )
    load(0).start()
    small = [
        pltpu.make_async_copy(far, near, small_sem.at[k])
        for k, (far, near) in enumerate(
            (
                (day_far, day_ref),
                (foot_far, foot_ref),
                (offs_far, offs_ref),
                (foot_far, foot_rows),
                (offs_far, offs_rows),
            )
        )
    ]
    for copy in small:
        copy.start()
    for k in range(1, chunks):
        load(k).start()
    smooth.start()
    for copy in small:
        copy.wait()

    table_ref[cover_row : cover_row + TABLE, 2 * cols : 3 * cols] = jnp.zeros((TABLE, cols), bf16)
    fit_tables(day_ref, table_ref, cover_row, 2 * cols)
    strip = lane_iota((8, cols), 1) // STRIP
    span = dates * 8 // 2
    lines[...] = jnp.zeros_like(lines)
    lines[0:2, :dates] = foot_rows[...].astype(f32)
    lines[2:4, :dates] = offs_rows[...].astype(f32) * (1.0 / 16.0)
    column = lines[...].T[:EDGES]
    first, last, fy, fx = (jnp.broadcast_to(column[:, k : k + 1], (EDGES, cols)) for k in range(4))
    lane = lane_iota((EDGES, cols), 1)
    here = (lane // STRIP).astype(f32)
    for k, entry in enumerate(
        (
            fy * (1.0 - fx),
            jnp.where(lane > 0, fy * fx, 0.0),
            jnp.where((here >= first) & (here <= last), 1.0, 0.0),
        )
    ):
        table_ref[cover_row + k * EDGES : cover_row + (k + 1) * EDGES, 3 * cols : 4 * cols] = entry.astype(bf16)

    for side in range(2):

        def cover(tp, carry, lane=side):
            tiles = []
            for u in (0, 1):
                t = lane * (span // 8) + 2 * tp + u
                inside = (strip >= foot_ref[0, t]) & (strip <= foot_ref[1, t])
                tiles.append(jnp.where(inside, 1.0, 0.0))
            row = pl.multiple_of(cover_row + 16 * tp, 16)
            table_ref[pl.ds(row, 16), lane * cols : (lane + 1) * cols] = jnp.concatenate(tiles, axis=0).astype(bf16)
            return carry

        lax.fori_loop(0, span // 16, cover, 0)
    used = cover_row + span
    smooth.wait()
    save_table = pltpu.make_async_copy(
        table_ref.at[pl.ds(0, used), :], table_far.at[pl.ds(0, used), :], out_sem.at[0]
    )
    save_table.start()

    not_last = lane_iota((8, cols), 1) < cols - 1
    bottom = lane_iota((8, cols), 0) == 7

    def splat(value):
        return jnp.full((8, cols), value, jnp.int32).astype(f32) * (1.0 / 16.0)

    def pair(tp, carry):
        fractions = []
        for u in (0, 1):
            t = 2 * tp + u
            fy, fx = splat(offs_ref[0, t]), splat(offs_ref[1, t])
            fractions.append((fy, 1.0 - fy, 1.0 - fx, jnp.where(not_last, fx, 0.0)))
        for s in range(bands):
            halves = []
            for u in (0, 1):
                fy, gy, keep, take = fractions[u]
                source = scene[2 * tp + u, s].astype(f32)
                across = []
                for part in range(parts):
                    piece = source[8 * part : 8 * part + 8]
                    across.append(keep * piece + take * pltpu.roll(piece, cols - 1, 1))
                turned = [pltpu.roll(piece, 7, 0) for piece in across]
                turned.append(0.0)
                halves.append(
                    [
                        gy * across[part] + fy * jnp.where(bottom, turned[part + 1], turned[part])
                        for part in range(parts)
                    ]
                )
            for part in range(parts):
                tile = jnp.concatenate([halves[0][part], halves[1][part]], axis=0)
                x_ref[part, s, pl.ds(pl.multiple_of(16 * tp, 16), 16), :] = tile.astype(bf16)
        return carry

    def save(k):
        inner = pl.ds(k * chunk * 8, chunk * 8)
        return pltpu.make_async_copy(x_ref.at[:, :, inner, :], x_far.at[:, :, inner, :], out_sem.at[1 + k])

    for k in range(chunks):
        load(k).wait()
        lax.fori_loop(k * chunk // 2, (k + 1) * chunk // 2, pair, 0)
        save(k).start()
    save_table.wait()
    for k in range(chunks):
        save(k).wait()


def fit_body(
    words,
    place_ref,
    bits_ref,
    below_ref,
    x_far,
    table_far,
    send_ref,
    x_ref,
    table_ref,
    below_wide,
    edge_ref,
    b8,
    bfull,
    wc_ref,
    w_ref,
    g_ref,
    inv_ref,
    wide_ref,
    y_ref,
    in_sem,
):
    f32, bf16 = jnp.float32, jnp.bfloat16
    dates, bands, cols = below_ref.shape
    cells_here = b8.shape[1]
    steps, _, _, wide = bfull.shape
    group = wide // cols
    parts = steps * group
    rows = 8 * parts
    half = cells_here // parts
    depth, width = 8 * dates, table_ref.shape[1]
    smooth_row = TABLE + PRODUCT
    cover_row = smooth_row + 2 * cols
    span = depth // words
    arrivals = [
        pltpu.make_async_copy(far, near, in_sem.at[k])
        for k, (far, near) in enumerate(
            (
                (table_far.at[pl.ds(cover_row, span), :], table_ref.at[pl.ds(cover_row, span), :]),
                (table_far.at[pl.ds(0, cover_row), :], table_ref.at[pl.ds(0, cover_row), :]),
                (x_far, x_ref),
            )
        )
    ]
    for copy in arrivals:
        copy.start()

    own_words(words, place_ref[0] * cells_here, bits_ref, b8)
    y_ref[...] = jnp.zeros_like(y_ref)
    top = lane_iota((8, cols), 0) < 8 // half
    for w in range(words):
        for part in range(parts):
            q, g = divmod(part, group)
            bfull[q, w, :, g * cols : (g + 1) * cols] = jnp.where(
                top, b8[w, part * half : part * half + 1, :], b8[w, part * half + 1 : part * half + 2, :]
            )

    def spread_rows(t, carry):
        below_wide[pl.ds(pl.multiple_of(8 * t, 8), bands), :] = below_ref[t].astype(f32)
        return carry

    lax.fori_loop(0, dates, spread_rows, 0)
    arrivals[0].wait()
    per_word = dates // words
    when = lane_iota((EDGES, cols), 0)
    word = b8[0, cells_here - 1 : cells_here, :]
    for w in range(1, words):
        word = jnp.where(when >= w * per_word, b8[w, cells_here - 1 : cells_here, :], word)
    flag = (lax.shift_right_logical(jnp.broadcast_to(word, (EDGES, cols)), when % per_word) & 1).astype(f32)
    near, far, cover = (
        table_ref[cover_row + k * EDGES : cover_row + (k + 1) * EDGES, 3 * cols : 4 * cols].astype(f32)
        for k in range(3)
    )
    flag = flag * cover
    near, far = near * flag, far
    for s in range(bands):
        row = below_wide[pl.ds(s, EDGES, stride=8), :]
        edge = near * row + flag * pltpu.roll(far * row, cols - 1, 1)
        edge_ref[s] = jnp.where(when < dates, edge, 0.0).astype(bf16)
    for lane in range(words):

        def mask_pair(tp, carry, lane=lane):
            cover = table_ref[pl.ds(pl.multiple_of(cover_row + 16 * tp, 16), 16), lane * cols : (lane + 1) * cols]
            first = lane * (span // 8) + 2 * tp
            w = first // per_word
            coarse = b8[w]
            fine = [bfull[q, w] for q in range(steps)]
            small, large = [], [[] for _ in range(steps)]
            for u in (0, 1):
                bit = jnp.left_shift(1, first + u - w * per_word)
                small.append(jnp.where((coarse & bit) != 0, 1.0, 0.0))
                for q in range(steps):
                    large[q].append(jnp.where((fine[q] & bit) != 0, 1.0, 0.0))
            row = pl.ds(pl.multiple_of(lane * span + 16 * tp, 16), 16)
            wc_ref[row, :] = jnp.concatenate(small, axis=0).astype(bf16) * cover
            for q in range(steps):
                both = jnp.concatenate(large[q], axis=0).astype(bf16)
                w_ref[q, row, :] = both * jnp.concatenate([cover] * group, axis=1)
            return carry

        lax.fori_loop(0, span // 16, mask_pair, 0)
    arrivals[1].wait()
    g_ref[...] = jnp.dot(table_ref[TABLE:smooth_row, :depth], wc_ref[...], preferred_element_type=f32)
    solve_cells(g_ref, inv_ref)

    def widen(block, carry):
        for k in range(7):
            n = 7 * block + k
            for part in range(parts):
                q, g = divmod(part, group)
                wide_ref[q, n, :, g * cols : (g + 1) * cols] = jnp.where(
                    top,
                    inv_ref[n, part * half : part * half + 1, :],
                    inv_ref[n, part * half + 1 : part * half + 2, :],
                )
        return carry

    lax.fori_loop(0, inv_ref.shape[0] // 7, widen, 0)

    arrivals[2].wait()

    coef_groups = cdiv(8 * bands, 16)
    order = {}
    for i in range(8):
        for j in range(i + 1):
            order[i, j] = order[j, i] = len(set(order.values()))

    def sums_of(q, s):
        weighted = jnp.concatenate([x_ref[q * group + g, s] for g in range(group)], axis=1) * w_ref[q]
        sums = jnp.dot(table_ref[:TABLE, :depth], weighted, preferred_element_type=f32)
        if q == steps - 1:
            edge = jnp.concatenate([jnp.zeros((EDGES, (group - 1) * cols), bf16), edge_ref[s]], axis=1)
            near_edge = table_ref[cover_row : cover_row + TABLE, 2 * cols : 2 * cols + EDGES]
            sums = sums + jnp.dot(near_edge, edge, preferred_element_type=f32)
        return sums

    def put(q, base, e, u, value):
        tall = jnp.concatenate([value[:, g * cols : (g + 1) * cols] for g in range(group)], axis=0)
        row = u % 8 * rows + q * group * 8
        y_ref[base + u // 8, row : row + group * 8, e * cols : (e + 1) * cols] = tall.astype(bf16)

    def use(q, s, sums):
        month = [sums[8 * (14 + m) : 8 * (14 + m) + 8] for m in range(12)]
        whole = month[0]
        for m in range(1, 12):
            whole = whole + month[m]
        rhs = [whole] + [sums[8 * k : 8 * k + 8] + sums[8 * (k + 7) : 8 * (k + 7) + 8] for k in range(7)]
        for m in range(12):
            put(q, coef_groups, m % 2, (m // 2) * bands + s, month[m] * wide_ref[q, 36 + m])
        put(q, coef_groups, s % 2, 6 * bands + s // 2, whole * wide_ref[q, 48])
        for i in range(8):
            value = wide_ref[q, order[i, 0]] * rhs[0]
            for j in range(1, 8):
                value = value + wide_ref[q, order[i, j]] * rhs[j]
            put(q, 0, i % 2, (i // 2) * bands + s, value)

    places = [(q, s) for q in range(steps) for s in range(bands)]
    waiting = sums_of(*places[0])
    for n, (q, s) in enumerate(places):
        ready = waiting
        if n + 1 < len(places):
            waiting = sums_of(*places[n + 1])
        use(q, s, ready)

    for at in range(y_ref.shape[0]):
        side = 0 if at < coef_groups else 2 * cols
        turned = lax.dot_general(
            table_ref[smooth_row:cover_row, side : side + 2 * cols],
            y_ref[at],
            (((1,), (1,)), ((), ())),
            preferred_element_type=f32,
        ).reshape(cols // STRIP, 2 * STRIP, 2 * cols)
        tile = jnp.concatenate([turned[:, :, :cols], turned[:, :, cols:]], axis=1)
        send_ref[:, 16 * at : 16 * at + 16, :] = tile.astype(bf16)


def finish_body(bands, recv_ref, coef_ref, month_ref, year_ref, field_ref, out_sem):
    strips, slots, lanes = recv_ref.shape
    groups = slots // 16
    coef_groups = cdiv(8 * bands, 16)
    quarter = lanes // 4
    lane = lane_iota((16, lanes), 1)
    low_half = lane < 2 * quarter
    even = lane // quarter % 2 == 0

    def save(k):
        first, count, target = (
            (0, 8 * bands, coef_ref),
            (8 * bands, 8 * bands, month_ref.at[pl.ds(0, 8 * bands)]),
            (16 * bands, 4 * bands, month_ref.at[pl.ds(8 * bands, 4 * bands)]),
            (20 * bands, bands, year_ref),
        )[k]
        return pltpu.make_async_copy(field_ref.at[pl.ds(first, count)], target, out_sem.at[k])

    def one_group(is_coef, at, carry):
        part = pl.ds(pl.multiple_of(16 * at, 16), 16)
        tiles = []
        for lt in range(strips // 4):
            x = [recv_ref[4 * lt + b, part, :] for b in range(4)]
            for b in (0, 1):
                first, second = x[b], x[b + 2]
                x[b] = jnp.where(low_half, first, pltpu.roll(second, 2 * quarter, 1))
                x[b + 2] = jnp.where(low_half, pltpu.roll(first, 2 * quarter, 1), second)
            for b in (0, 2):
                first, second = x[b], x[b + 1]
                x[b] = jnp.where(even, first, pltpu.roll(second, quarter, 1))
                x[b + 1] = jnp.where(even, pltpu.roll(first, 3 * quarter, 1), second)
            tiles.append(x)
        for p in range(4):
            field = jnp.concatenate([tile[p].astype(jnp.float32) for tile in tiles], axis=1)
            if not is_coef:
                full = field.shape[1]
                where = lane_iota(field.shape, 1)
                before = jnp.where(where == 0, 0.0, pltpu.roll(field, 1, 1))
                after = jnp.where(where == full - 1, 0.0, pltpu.roll(field, full - 1, 1))
                field = 0.25 * before + 0.5 * field + 0.25 * after
            for h in (0, 1):
                u = 8 * at + 4 * h + p
                late = u - 8 * coef_groups
                for e in (0, 1):
                    coef = (2 * (u // bands) + e) * bands + lax.rem(u, bands)
                    month = (2 * (late // bands) + e) * bands + lax.rem(late, bands)
                    mean = 2 * (late - 6 * bands) + e
                    v = coef if is_coef else jnp.where(late < 6 * bands, 8 * bands + month, 20 * bands + mean)
                    field_ref[v] = field[8 * h + 4 * e : 8 * h + 4 * e + 4]
        return carry

    lax.fori_loop(0, coef_groups, functools.partial(one_group, True), 0)
    save(0).start()
    early = coef_groups + 4 * bands // 8
    lax.fori_loop(coef_groups, early, functools.partial(one_group, False), 0)
    save(1).start()
    lax.fori_loop(early, groups, functools.partial(one_group, False), 0)
    save(2).start()
    save(3).start()
    for k in range(4):
        save(k).wait()


def turn_tables(strips, strip_width):
    cols = strips * strip_width
    row, col = np.arange(2 * cols)[:, None], np.arange(2 * cols)[None, :]
    column = strip_width * (row // (2 * strip_width)) + row % strip_width
    same = row // strip_width % 2 == col // cols
    apart = np.abs(column - col % cols)
    plain = np.where(same & (apart == 0), 1.0, 0.0)
    smooth = np.where(same, np.where(apart == 0, 0.5, np.where(apart == 1, 0.25, 0.0)), 0.0)
    return jnp.asarray(np.concatenate([plain, smooth], axis=1), jnp.bfloat16)


def whole_dates(scenes, clear_bits, footprint, offsets, acq_day):
    dates, bands, rows, cols = scenes.shape
    words, _, cells = clear_bits.shape
    strips = lax.axis_size("band")
    cells_here = cells // strips
    group, lanes, chunks = 2, 128, 6
    steps = rows // 8 // group
    depth, wide = 8 * dates, group * cols
    f32, bf16 = jnp.float32, jnp.bfloat16
    blocks = words * cells // lanes
    flags = jnp.broadcast_to(clear_bits.reshape(1, blocks, 1, lanes), (strips, blocks, 1, lanes))
    flags = lax.all_to_all(flags, "band", split_axis=0, concat_axis=0, tiled=True)
    below = shifted(scenes[:, :, 0, :], "band", -1)
    smem = pl.BlockSpec(memory_space=pltpu.SMEM)
    vmem = pl.BlockSpec(memory_space=pltpu.VMEM)
    anywhere = pl.BlockSpec(memory_space=pl.ANY)
    groups = cdiv(8 * bands, 16) + cdiv(13 * bands, 16)
    place = lax.axis_index("band").reshape(1).astype(jnp.int32)
    parts, table_width = rows // 8, 4 * cols
    x_shape = (parts, bands, depth, cols)
    table_shape = (TABLE + PRODUCT + 4 * cols + 16, table_width)
    resampled, table = pl.pallas_call(
        resample_body,
        in_specs=[anywhere] * 5,
        out_specs=[anywhere] * 2,
        out_shape=[
            jax.ShapeDtypeStruct(x_shape, bf16),
            jax.ShapeDtypeStruct(table_shape, bf16),
        ],
        scratch_shapes=[
            pltpu.SMEM((2, dates), jnp.int32),
            pltpu.SMEM((2, dates), jnp.int32),
            pltpu.VMEM((1, dates), jnp.int32),
            pltpu.VMEM((2, dates), jnp.int32),
            pltpu.VMEM((2, dates), jnp.int32),
            pltpu.SemaphoreType.DMA((5,)),
            pltpu.VMEM(scenes.shape, bf16),
            pltpu.VMEM(x_shape, bf16),
            pltpu.VMEM(table_shape, bf16),
            pltpu.VMEM((8, 128), f32),
            pltpu.SemaphoreType.DMA((chunks + 1,)),
            pltpu.SemaphoreType.DMA((chunks + 1,)),
        ],
        cost_estimate=pl.CostEstimate(flops=20_000_000, bytes_accessed=9_000_000, transcendentals=0),
        name="resample",
    )(footprint.T, offsets.T, acq_day.reshape(1, dates), turn_tables(strips, STRIP), scenes)
    send = pl.pallas_call(
        functools.partial(fit_body, words),
        in_specs=[smem, vmem, vmem, anywhere, anywhere],
        out_specs=vmem,
        out_shape=jax.ShapeDtypeStruct((strips, 16 * groups, 4 * rows), bf16),
        scratch_shapes=[
            pltpu.VMEM(x_shape, bf16),
            pltpu.VMEM(table_shape, bf16),
            pltpu.VMEM((8 * EDGES, cols), f32),
            pltpu.VMEM((bands, EDGES, cols), bf16),
            pltpu.VMEM((words, cells_here, cols), jnp.int32),
            pltpu.VMEM((steps, words, 8, wide), jnp.int32),
            pltpu.VMEM((depth, cols), bf16),
            pltpu.VMEM((steps, depth, wide), bf16),
            pltpu.VMEM((PRODUCT, cols), f32),
            pltpu.VMEM((49, cells_here, cols), f32),
            pltpu.VMEM((steps, 49, 8, wide), f32),
            pltpu.VMEM((groups, 8 * rows, 2 * cols), bf16),
            pltpu.SemaphoreType.DMA((3,)),
        ],
        compiler_params=pltpu.CompilerParams(vmem_limit_bytes=FIT_VMEM),
        cost_estimate=pl.CostEstimate(flops=20_000_000, bytes_accessed=6_000_000, transcendentals=0),
        name="fit",
    )(place, flags.reshape(strips * blocks, lanes), below, resampled, table)
    received = lax.all_to_all(send, "band", split_axis=0, concat_axis=0, tiled=True)
    row_count = rows * strips
    shapes = [(n * bands, STRIP, row_count) for n in (8, 12, 1)]
    coefficients, monthly, annual = pl.pallas_call(
        functools.partial(finish_body, bands),
        in_specs=[vmem],
        out_specs=[anywhere] * 3,
        out_shape=[jax.ShapeDtypeStruct(shape, f32) for shape in shapes],
        scratch_shapes=[
            pltpu.VMEM((16 * groups, STRIP, row_count), f32),
            pltpu.SemaphoreType.DMA((4,)),
        ],
        compiler_params=pltpu.CompilerParams(vmem_limit_bytes=8 << 20),
        name="finish",
    )(received)
    return (
        coefficients.reshape(8, bands, STRIP, row_count),
        monthly.reshape(12, bands, STRIP, row_count),
        annual,
    )


def shards(scenes, clear_bits, footprint, offsets, acq_day):
    dates, bands, rows, cols = scenes.shape
    strips = lax.axis_size("band")
    words, _, cells = clear_bits.shape
    whole = (
        lax.axis_size("tile") == 1
        and cols == 128
        and rows == 32
        and cols == STRIP * strips
        and cells == 8 * strips
        and words == 2
        and dates == 30 * words
        and dates % 12 == 0
        and dates <= 60
        and bands % 6 == 0
        and bands <= 6
    )
    plan = whole_dates if whole else split_dates
    return plan(scenes, clear_bits, footprint, offsets, acq_day)


def solution(mesh):
    placed = (
        P(("region", "tile"), "sub", "band", None),
        P(("region", "tile"), "band", None),
        P(("region", "tile"), None),
        P(("region", "tile"), None),
        P(("region", "tile")),
    )
    return jax.shard_map(
        shards,
        mesh=mesh,
        in_specs=placed,
        out_specs=(
            P("region", "sub", "band", "tile"),
            P(("region", "tile"), "sub", "band", None),
            P(("region", "sub"), "band", "tile"),
        ),
        check_vma=False,
    )
```

profile of v0, /device:TPU:0, one launch (start us, length us, event | category | flops | bytes accessed | tf_op | source)
XLA Modules:
  0.0 59.3 jit_solution(16163882929624539181)
XLA Ops:
  0.6 1.3 %broadcast_in_dim.8 = s32[32,4,1,128]{3,1,2,0:T(4,128)} broadcast(s32[4,128]{1,0:T(4,128)} %bitcast.13), dimensions={1,3} | broadcast | bytes 67584 | tf_op jit(solution)/shard_map/broadcast_in_dim | solution.py:709
  1.9 7.3 %all-to-all-start = ((s32[32,4,1,128]{3,1,2,0:T(4,128)}), s32[32,4,1,128]{3,1,2,0:T(4,128)S(1)}, u32[]{:S(2)}, u32[]{:S(2)}) async-start(s32[32,4,1,128]{3,1,2,0:T(4,128)} %broadcast_in_dim.8), calls=%async_computation | async-start | bytes 131072 | tf_op jit(solution)/shard_map/all_to_all | solution.py:710
  9.3 1.2 %slice.3 = bf16[60,6,1,128]{3,2,1,0:T(2,128)(2,1)S(1)} slice(bf16[60,6,32,128]{3,2,1,0:T(8,128)(2,1)} %scene_far.1), slice={[0:60], [0:6], [0:1], [0:128]} | slice | bytes 184320 | tf_op jit(solution)/shard_map/slice | solution.py:711
  10.5 1.3 %collective-permute-start = (bf16[60,6,128]{2,1,0:T(8,128)(2,1)S(1)}, bf16[60,6,128]{2,1,0:T(8,128)(2,1)S(1)}, u32[]{:S(2)}, u32[]{:S(2)}) collective-permute-start(bf16[60,6,128]{2,1,0:T(8,128)(2,1)S(1)} %bitcast.12), channel_id=1, source_target_pairs={{1,0},{2,1},{3,2},{4,3},{5,4},{6,5},{7,6},{8,7},{9,8},{10,9},{11,1... | collective-permute-start | bytes 276488 | tf_op jit(solution)/shard_map/ppermute | solution.py:22
  11.8 7.2 %resample.1 = (bf16[4,6,480,128]{3,2,1,0:T(8,128)(2,1)}, bf16[1408,512]{1,0:T(8,128)(2,1)}) custom-call(s32[2,60]{1,0:T(2,128)} %bitcast.14, s32[2,60]{1,0:T(2,128)} %bitcast.15, s32[1,60]{1,0:T(1,128)} %bitcast.16, bf16[256,512]{1,0:T(8,128)(2,1)} %constant.6.clone.smooth_far, bf16[60,6,32,128]{3,2,1,0:T(8,128)(2,1)} %scene_far.1), custom_call_target="tpu_custom_call" | custom-call | flops 20000000 | bytes 9000000 | tf_op jit(solution)/shard_map/resample/pallas_call | solution.py:720
  19.1 0.0 collective-permute-done.below_ref
  19.1 0.0 all-to-all-done
  19.1 4.4 %fit.1 = bf16[32,128,128]{2,1,0:T(8,128)(2,1)S(1)} custom-call(s32[1]{0:T(128)} %bitcast.place_ref, s32[128,128]{1,0:T(8,128)S(1)} %bitcast.11, bf16[60,6,128]{2,1,0:T(8,128)(2,1)S(1)} %collective-permute-done.below_ref, bf16[4,6,480,128]{3,2,1,0:T(8,128)(2,1)} %get-tuple-element.8.x_far, bf16[1408,512]{1,0:T(8,128)(2,1)} %get-tuple-element.9.table_far), custom_call_target="tpu_custom_call" | custom-call | flops 20000000 | bytes 6000000 | tf_op jit(solution)/shard_map/fit/pallas_call | solution.py:745
  23.5 32.7 %all_to_all.10.recv_ref = bf16[32,128,128]{2,1,0:T(8,128)(2,1)S(1)} all-to-all(bf16[32,128,128]{2,1,0:T(8,128)(2,1)S(1)} %fit.1), channel_id=1, replica_groups=mesh['region'=1,'band'=32,'tile'=1,'sub'=1] {'band'}, dimensions={0} | all-to-all | bytes 2097152 | tf_op jit(solution)/shard_map/all_to_all | solution.py:769
  56.2 3.0 %finish.1 = (f32[48,4,1024]{2,1,0:T(4,128)}, f32[72,4,1024]{2,1,0:T(4,128)}, f32[6,4,1024]{2,1,0:T(4,128)}) custom-call(bf16[32,128,128]{2,1,0:T(8,128)(2,1)S(1)} %all_to_all.10.recv_ref), custom_call_target="tpu_custom_call" | custom-call | tf_op jit(solution)/shard_map/finish/pallas_call | solution.py:772
  (1 shorter events, 0.0 us)
Async XLA Ops:
  1.9 17.2 %all-to-all-start = ((s32[32,4,1,128]{3,1,2,0:T(4,128)}), s32[32,4,1,128]{3,1,2,0:T(4,128)S(1)}, u32[]{:S(2)}, u32[]{:S(2)}) async-start(s32[32,4,1,128]{3,1,2,0:T(4,128)} %broadcast_in_dim.8), calls=%async_computation | async-start | bytes 131072 | tf_op jit(solution)/shard_map/all_to_all | solution.py:710
  10.5 8.6 %collective-permute-start = (bf16[60,6,128]{2,1,0:T(8,128)(2,1)S(1)}, bf16[60,6,128]{2,1,0:T(8,128)(2,1)S(1)}, u32[]{:S(2)}, u32[]{:S(2)}) collective-permute-start(bf16[60,6,128]{2,1,0:T(8,128)(2,1)S(1)} %bitcast.12), channel_id=1, source_target_pairs={{1,0},{2,1},{3,2},{4,3},{5,4},{6,5},{7,6},{8,7},{9,8},{10,9},{11,1... | collective-permute-start | bytes 276488 | tf_op jit(solution)/shard_map/ppermute | solution.py:22
where the time goes:
time: 59.6 us; the launch traced here: 59.3 us
  blocking collectives  32.7 us (55%)
  Pallas kernels  14.7 us (25%)
  starting transfers between devices  8.62 us (14%)
  local copies, waits for them, and re-layouts  2.57 us (4%)
  between operations  0.69 us (1%)
    all_to_all x1, blocking collectives, whole_dates(): lax.all_to_all(send, 'band', split_axis=0, concat_axis=0, tiled=True)  32.7 us
    all_to_all x1, starting transfers between devices, whole_dates(): lax.all_to_all(flags, 'band', split_axis=0, concat_axis=0, tiled=True)  7.33 us
    pallas_call x1, Pallas kernels, whole_dates(): pl.pallas_call(resample_body, in_specs=[anywhere] * 5, out_specs=[anywher...  7.25 us
    pallas_call x1, Pallas kernels, whole_dates(): pl.pallas_call(functools.partial(fit_body, words), in_specs=[smem, vmem,...  4.37 us
    pallas_call x1, Pallas kernels, whole_dates(): pl.pallas_call(functools.partial(finish_body, bands), in_specs=[vmem], ou...  3.05 us
    broadcast_in_dim x1, local copies, waits for them, and re-layouts, whole_dates(): jnp.broadcast_to(clear_bits.reshape(1, blocks, 1, lanes), (strips, blocks...  1.32 us
    ppermute x1, starting transfers between devices, shifted(): lax.ppermute(value, axis, [(source, source + steps) for source in range(f...  1.29 us
    slice x1, local copies, waits for them, and re-layouts, whole_dates(): below = shifted(scenes[:, :, 0, :], 'band', -1)  1.22 us
  transfers between devices with their start and end apart: 2, of which 0 were waited for; matrix products, arithmetic and copies ran while one was open for 2% of the time, Pallas kernels for 12%

commit v1 on v0

--- a/solution.py
+++ b/solution.py
@@ -13,7 +13,8 @@
 TABLE = 8 * 26
 PRODUCT = 8 * 84
 EDGES = 64
-FIT_VMEM = 60 * 1024 * 1024 - (8 << 20)
+RESAMPLE_VMEM = 16 << 20
+FIT_VMEM = 20 << 20
 
 
 def shifted(value, axis, steps):
@@ -307,7 +308,7 @@
     day_far,
     smooth_far,
     scene_far,
-    x_far,
+    x_ref,
     table_far,
     foot_ref,
     offs_ref,
@@ -316,7 +317,6 @@
     offs_rows,
     small_sem,
     scene,
-    x_ref,
     table_ref,
     lines,
     in_sem,
@@ -415,11 +415,13 @@
             halves = []
             for u in (0, 1):
                 fy, gy, keep, take = fractions[u]
-                source = scene[2 * tp + u, s].astype(f32)
+                raw = scene[2 * tp + u, s]
+                source = raw.astype(f32)
+                beside = pltpu.roll(raw, cols - 1, 1).astype(f32)
                 across = []
                 for part in range(parts):
                     piece = source[8 * part : 8 * part + 8]
-                    across.append(keep * piece + take * pltpu.roll(piece, cols - 1, 1))
+                    across.append(keep * piece + take * beside[8 * part : 8 * part + 8])
                 turned = [pltpu.roll(piece, 7, 0) for piece in across]
                 turned.append(0.0)
                 halves.append(
@@ -433,17 +435,10 @@
                 x_ref[part, s, pl.ds(pl.multiple_of(16 * tp, 16), 16), :] = tile.astype(bf16)
         return carry
 
-    def save(k):
-        inner = pl.ds(k * chunk * 8, chunk * 8)
-        return pltpu.make_async_copy(x_ref.at[:, :, inner, :], x_far.at[:, :, inner, :], out_sem.at[1 + k])
-
     for k in range(chunks):
         load(k).wait()
         lax.fori_loop(k * chunk // 2, (k + 1) * chunk // 2, pair, 0)
-        save(k).start()
     save_table.wait()
-    for k in range(chunks):
-        save(k).wait()
 
 
 def fit_body(
@@ -451,10 +446,9 @@
     place_ref,
     bits_ref,
     below_ref,
-    x_far,
+    x_ref,
     table_far,
     send_ref,
-    x_ref,
     table_ref,
     below_wide,
     edge_ref,
@@ -481,14 +475,8 @@
     cover_row = smooth_row + 2 * cols
     span = depth // words
     arrivals = [
-        pltpu.make_async_copy(far, near, in_sem.at[k])
-        for k, (far, near) in enumerate(
-            (
-                (table_far.at[pl.ds(cover_row, span), :], table_ref.at[pl.ds(cover_row, span), :]),
-                (table_far.at[pl.ds(0, cover_row), :], table_ref.at[pl.ds(0, cover_row), :]),
-                (x_far, x_ref),
-            )
-        )
+        pltpu.make_async_copy(table_far.at[part, :], table_ref.at[part, :], in_sem.at[k])
+        for k, part in enumerate((pl.ds(cover_row, span), pl.ds(0, cover_row)))
     ]
     for copy in arrivals:
         copy.start()
@@ -565,7 +553,6 @@
 
     lax.fori_loop(0, inv_ref.shape[0] // 7, widen, 0)
 
-    arrivals[2].wait()
 
     coef_groups = cdiv(8 * bands, 16)
     order = {}
@@ -701,7 +688,7 @@
     words, _, cells = clear_bits.shape
     strips = lax.axis_size("band")
     cells_here = cells // strips
-    group, lanes, chunks = 2, 128, 6
+    group, lanes, chunks = 2, 128, 3
     steps = rows // 8 // group
     depth, wide = 8 * dates, group * cols
     f32, bf16 = jnp.float32, jnp.bfloat16
@@ -712,18 +699,22 @@
     smem = pl.BlockSpec(memory_space=pltpu.SMEM)
     vmem = pl.BlockSpec(memory_space=pltpu.VMEM)
     anywhere = pl.BlockSpec(memory_space=pl.ANY)
+    far = pl.BlockSpec(memory_space=pltpu.HBM)
     groups = cdiv(8 * bands, 16) + cdiv(13 * bands, 16)
     place = lax.axis_index("band").reshape(1).astype(jnp.int32)
     parts, table_width = rows // 8, 4 * cols
     x_shape = (parts, bands, depth, cols)
     table_shape = (TABLE + PRODUCT + 4 * cols + 16, table_width)
+    def pinned(x):
+        return pltpu.with_memory_space_constraint(x, pltpu.HBM)
+
     resampled, table = pl.pallas_call(
         resample_body,
-        in_specs=[anywhere] * 5,
-        out_specs=[anywhere] * 2,
+        in_specs=[far] * 5,
+        out_specs=[vmem, far],
         out_shape=[
             jax.ShapeDtypeStruct(x_shape, bf16),
-            jax.ShapeDtypeStruct(table_shape, bf16),
+            pltpu.HBM(table_shape, bf16),
         ],
         scratch_shapes=[
             pltpu.SMEM((2, dates), jnp.int32),
@@ -733,22 +724,21 @@
             pltpu.VMEM((2, dates), jnp.int32),
             pltpu.SemaphoreType.DMA((5,)),
             pltpu.VMEM(scenes.shape, bf16),
-            pltpu.VMEM(x_shape, bf16),
             pltpu.VMEM(table_shape, bf16),
             pltpu.VMEM((8, 128), f32),
             pltpu.SemaphoreType.DMA((chunks + 1,)),
-            pltpu.SemaphoreType.DMA((chunks + 1,)),
+            pltpu.SemaphoreType.DMA((1,)),
         ],
+        compiler_params=pltpu.CompilerParams(vmem_limit_bytes=RESAMPLE_VMEM),
         cost_estimate=pl.CostEstimate(flops=20_000_000, bytes_accessed=9_000_000, transcendentals=0),
         name="resample",
-    )(footprint.T, offsets.T, acq_day.reshape(1, dates), turn_tables(strips, STRIP), scenes)
+    )(*(pinned(x) for x in (footprint.T, offsets.T, acq_day.reshape(1, dates), turn_tables(strips, STRIP), scenes)))
     send = pl.pallas_call(
         functools.partial(fit_body, words),
-        in_specs=[smem, vmem, vmem, anywhere, anywhere],
+        in_specs=[smem, vmem, vmem, vmem, far],
         out_specs=vmem,
         out_shape=jax.ShapeDtypeStruct((strips, 16 * groups, 4 * rows), bf16),
         scratch_shapes=[
-            pltpu.VMEM(x_shape, bf16),
             pltpu.VMEM(table_shape, bf16),
             pltpu.VMEM((8 * EDGES, cols), f32),
             pltpu.VMEM((bands, EDGES, cols), bf16),
@@ -760,12 +750,12 @@
             pltpu.VMEM((49, cells_here, cols), f32),
             pltpu.VMEM((steps, 49, 8, wide), f32),
             pltpu.VMEM((groups, 8 * rows, 2 * cols), bf16),
-            pltpu.SemaphoreType.DMA((3,)),
+            pltpu.SemaphoreType.DMA((2,)),
         ],
         compiler_params=pltpu.CompilerParams(vmem_limit_bytes=FIT_VMEM),
         cost_estimate=pl.CostEstimate(flops=20_000_000, bytes_accessed=6_000_000, transcendentals=0),
         name="fit",
-    )(place, flags.reshape(strips * blocks, lanes), below, resampled, table)
+    )(place, flags.reshape(strips * blocks, lanes), below, resampled, pinned(table))
     received = lax.all_to_all(send, "band", split_axis=0, concat_axis=0, tiled=True)
     row_count = rows * strips
     shapes = [(n * bands, STRIP, row_count) for n in (8, 12, 1)]

time: 59.6 us -> 58.7 us (0.985)
  Pallas kernels: 14.7 us -> 13.8 us
    pallas_call x1, Pallas kernels: 7.25 us -> 6.35 us  [whole_dates(): pl.pallas_call(resample_body, in_specs=[far] * 5, out_specs=[vmem, far],...]
  transfers between devices with their start and end apart: 2 -> 2, of which waited for: 0 -> 0; matrix products, arithmetic and copies ran while one was open for 2% -> 2% of each run, Pallas kernels for 12% -> 11%
where the time goes in v1:
time: 58.7 us; the launch traced here: 58.4 us
  blocking collectives  32.7 us (56%)
  Pallas kernels  13.8 us (24%)
  starting transfers between devices  8.62 us (15%)
  local copies, waits for them, and re-layouts  2.57 us (4%)
  between operations  0.69 us (1%)
    all_to_all x1, blocking collectives, whole_dates(): lax.all_to_all(send, 'band', split_axis=0, concat_axis=0, tiled=True)  32.7 us
    all_to_all x1, starting transfers between devices, whole_dates(): lax.all_to_all(flags, 'band', split_axis=0, concat_axis=0, tiled=True)  7.33 us
    pallas_call x1, Pallas kernels, whole_dates(): pl.pallas_call(resample_body, in_specs=[far] * 5, out_specs=[vmem, far],...  6.35 us
    pallas_call x1, Pallas kernels, whole_dates(): pl.pallas_call(functools.partial(fit_body, words), in_specs=[smem, vmem,...  4.36 us
    pallas_call x1, Pallas kernels, whole_dates(): pl.pallas_call(functools.partial(finish_body, bands), in_specs=[vmem], ou...  3.05 us
    broadcast_in_dim x1, local copies, waits for them, and re-layouts, whole_dates(): jnp.broadcast_to(clear_bits.reshape(1, blocks, 1, lanes), (strips, blocks...  1.32 us
    ppermute x1, starting transfers between devices, shifted(): lax.ppermute(value, axis, [(source, source + steps) for source in range(f...  1.29 us
    slice x1, local copies, waits for them, and re-layouts, whole_dates(): below = shifted(scenes[:, :, 0, :], 'band', -1)  1.22 us
  transfers between devices with their start and end apart: 2, of which 0 were waited for; matrix products, arithmetic and copies ran while one was open for 2% of the time, Pallas kernels for 11%

profile of v1, /device:TPU:0, one launch (start us, length us, event | category | flops | bytes accessed | tf_op | source)
XLA Modules:
  0.0 58.4 jit_solution(11959686411752760846)
XLA Ops:
  0.6 1.3 %broadcast_in_dim.8 = s32[32,4,1,128]{3,1,2,0:T(4,128)} broadcast(s32[4,128]{1,0:T(4,128)} %bitcast.13), dimensions={1,3} | broadcast | bytes 67584 | tf_op jit(solution)/shard_map/broadcast_in_dim | solution.py:696
  1.9 7.3 %all-to-all-start = ((s32[32,4,1,128]{3,1,2,0:T(4,128)}), s32[32,4,1,128]{3,1,2,0:T(4,128)S(1)}, u32[]{:S(2)}, u32[]{:S(2)}) async-start(s32[32,4,1,128]{3,1,2,0:T(4,128)} %broadcast_in_dim.8), calls=%async_computation | async-start | bytes 131072 | tf_op jit(solution)/shard_map/all_to_all | solution.py:697
  9.3 1.2 %slice.3 = bf16[60,6,1,128]{3,2,1,0:T(2,128)(2,1)S(1)} slice(bf16[60,6,32,128]{3,2,1,0:T(8,128)(2,1)} %scene_far.1), slice={[0:60], [0:6], [0:1], [0:128]} | slice | bytes 184320 | tf_op jit(solution)/shard_map/slice | solution.py:698
  10.5 1.3 %collective-permute-start = (bf16[60,6,128]{2,1,0:T(8,128)(2,1)S(1)}, bf16[60,6,128]{2,1,0:T(8,128)(2,1)S(1)}, u32[]{:S(2)}, u32[]{:S(2)}) collective-permute-start(bf16[60,6,128]{2,1,0:T(8,128)(2,1)S(1)} %bitcast.12), channel_id=1, source_target_pairs={{1,0},{2,1},{3,2},{4,3},{5,4},{6,5},{7,6},{8,7},{9,8},{10,9},{11,1... | collective-permute-start | bytes 276488 | tf_op jit(solution)/shard_map/ppermute | solution.py:23
  11.8 6.3 %resample.1 = (bf16[4,6,480,128]{3,2,1,0:T(8,128)(2,1)S(1)}, bf16[1408,512]{1,0:T(8,128)(2,1)}) custom-call(s32[2,60]{1,0:T(2,128)} %bitcast.14, s32[2,60]{1,0:T(2,128)} %bitcast.15, s32[1,60]{1,0:T(1,128)} %bitcast.16, bf16[256,512]{1,0:T(8,128)(2,1)} %constant.6.clone.smooth_far, bf16[60,6,32,128]{3,2,1,0:T(8,128)(2,1)} %scene_far.1), custom_call_target="tpu_custom_call" | custom-call | flops 20000000 | bytes 9000000 | tf_op jit(solution)/shard_map/resample/pallas_call | solution.py:711
  18.2 0.0 collective-permute-done.below_ref
  18.2 0.0 all-to-all-done
  18.2 4.4 %fit.1 = bf16[32,128,128]{2,1,0:T(8,128)(2,1)S(1)} custom-call(s32[1]{0:T(128)} %bitcast.place_ref, s32[128,128]{1,0:T(8,128)S(1)} %bitcast.11, bf16[60,6,128]{2,1,0:T(8,128)(2,1)S(1)} %collective-permute-done.below_ref, bf16[4,6,480,128]{3,2,1,0:T(8,128)(2,1)S(1)} %get-tuple-element.8.x_ref, bf16[1408,512]{1,0:T(8,128)(2,1)} %get-tuple-element.9.table_far), custom_call_target="tpu_custom_call" | custom-call | flops 20000000 | bytes 6000000 | tf_op jit(solution)/shard_map/fit/pallas_call | solution.py:736
  22.6 32.7 %all_to_all.10.recv_ref = bf16[32,128,128]{2,1,0:T(8,128)(2,1)S(1)} all-to-all(bf16[32,128,128]{2,1,0:T(8,128)(2,1)S(1)} %fit.1), channel_id=1, replica_groups=mesh['region'=1,'band'=32,'tile'=1,'sub'=1] {'band'}, dimensions={0} | all-to-all | bytes 2097152 | tf_op jit(solution)/shard_map/all_to_all | solution.py:759
  55.3 3.0 %finish.1 = (f32[48,4,1024]{2,1,0:T(4,128)}, f32[72,4,1024]{2,1,0:T(4,128)}, f32[6,4,1024]{2,1,0:T(4,128)}) custom-call(bf16[32,128,128]{2,1,0:T(8,128)(2,1)S(1)} %all_to_all.10.recv_ref), custom_call_target="tpu_custom_call" | custom-call | tf_op jit(solution)/shard_map/finish/pallas_call | solution.py:762
  (1 shorter events, 0.0 us)
Async XLA Ops:
  1.9 16.3 %all-to-all-start = ((s32[32,4,1,128]{3,1,2,0:T(4,128)}), s32[32,4,1,128]{3,1,2,0:T(4,128)S(1)}, u32[]{:S(2)}, u32[]{:S(2)}) async-start(s32[32,4,1,128]{3,1,2,0:T(4,128)} %broadcast_in_dim.8), calls=%async_computation | async-start | bytes 131072 | tf_op jit(solution)/shard_map/all_to_all | solution.py:697
  10.5 7.7 %collective-permute-start = (bf16[60,6,128]{2,1,0:T(8,128)(2,1)S(1)}, bf16[60,6,128]{2,1,0:T(8,128)(2,1)S(1)}, u32[]{:S(2)}, u32[]{:S(2)}) collective-permute-start(bf16[60,6,128]{2,1,0:T(8,128)(2,1)S(1)} %bitcast.12), channel_id=1, source_target_pairs={{1,0},{2,1},{3,2},{4,3},{5,4},{6,5},{7,6},{8,7},{9,8},{10,9},{11,1... | collective-permute-start | bytes 276488 | tf_op jit(solution)/shard_map/ppermute | solution.py:23

commit v2 on v1

--- a/solution.py
+++ b/solution.py
@@ -381,7 +381,7 @@
 
     for side in range(2):
 
-        def cover(tp, carry, lane=side):
+        def cover(tp, lane=side):
             tiles = []
             for u in (0, 1):
                 t = lane * (span // 8) + 2 * tp + u
@@ -389,9 +389,13 @@
                 tiles.append(jnp.where(inside, 1.0, 0.0))
             row = pl.multiple_of(cover_row + 16 * tp, 16)
             table_ref[pl.ds(row, 16), lane * cols : (lane + 1) * cols] = jnp.concatenate(tiles, axis=0).astype(bf16)
+
+        def covers(n, carry):
+            for k in range(3):
+                cover(3 * n + k)
             return carry
 
-        lax.fori_loop(0, span // 16, cover, 0)
+        lax.fori_loop(0, span // 48, covers, 0)
     used = cover_row + span
     smooth.wait()
     save_table = pltpu.make_async_copy(
@@ -482,7 +486,7 @@
         copy.start()
 
     own_words(words, place_ref[0] * cells_here, bits_ref, b8)
-    y_ref[...] = jnp.zeros_like(y_ref)
+    y_ref[y_ref.shape[0] - 1] = jnp.zeros(y_ref.shape[1:], bf16)
     top = lane_iota((8, cols), 0) < 8 // half
     for w in range(words):
         for part in range(parts):
@@ -491,11 +495,13 @@
                 top, b8[w, part * half : part * half + 1, :], b8[w, part * half + 1 : part * half + 2, :]
             )
 
-    def spread_rows(t, carry):
-        below_wide[pl.ds(pl.multiple_of(8 * t, 8), bands), :] = below_ref[t].astype(f32)
+    def spread_rows(n, carry):
+        for k in range(6):
+            t = 6 * n + k
+            below_wide[pl.ds(pl.multiple_of(8 * t, 8), bands), :] = below_ref[t].astype(f32)
         return carry
 
-    lax.fori_loop(0, dates, spread_rows, 0)
+    lax.fori_loop(0, dates // 6, spread_rows, 0)
     arrivals[0].wait()
     per_word = dates // words
     when = lane_iota((EDGES, cols), 0)
@@ -515,7 +521,7 @@
         edge_ref[s] = jnp.where(when < dates, edge, 0.0).astype(bf16)
     for lane in range(words):
 
-        def mask_pair(tp, carry, lane=lane):
+        def mask_pair(tp, lane=lane):
             cover = table_ref[pl.ds(pl.multiple_of(cover_row + 16 * tp, 16), 16), lane * cols : (lane + 1) * cols]
             first = lane * (span // 8) + 2 * tp
             w = first // per_word
@@ -532,9 +538,13 @@
             for q in range(steps):
                 both = jnp.concatenate(large[q], axis=0).astype(bf16)
                 w_ref[q, row, :] = both * jnp.concatenate([cover] * group, axis=1)
+
+        def mask_pairs(n, carry):
+            for k in range(3):
+                mask_pair(3 * n + k)
             return carry
 
-        lax.fori_loop(0, span // 16, mask_pair, 0)
+        lax.fori_loop(0, span // 48, mask_pairs, 0)
     arrivals[1].wait()
     g_ref[...] = jnp.dot(table_ref[TABLE:smooth_row, :depth], wc_ref[...], preferred_element_type=f32)
     solve_cells(g_ref, inv_ref)

time: 58.7 us -> 58.3 us (level)
  no operation moved by 1% of the time
where the time goes in v2:
time: 58.3 us; the launch traced here: 58 us
  blocking collectives  32.7 us (56%)
  Pallas kernels  13.3 us (23%)
  starting transfers between devices  8.62 us (15%)
  local copies, waits for them, and re-layouts  2.57 us (4%)
  between operations  0.69 us (1%)
    all_to_all x1, blocking collectives, whole_dates(): lax.all_to_all(send, 'band', split_axis=0, concat_axis=0, tiled=True)  32.7 us
    all_to_all x1, starting transfers between devices, whole_dates(): lax.all_to_all(flags, 'band', split_axis=0, concat_axis=0, tiled=True)  7.33 us
    pallas_call x1, Pallas kernels, whole_dates(): pl.pallas_call(resample_body, in_specs=[far] * 5, out_specs=[vmem, far],...  6.22 us
    pallas_call x1, Pallas kernels, whole_dates(): pl.pallas_call(functools.partial(fit_body, words), in_specs=[smem, vmem,...  4.08 us
    pallas_call x1, Pallas kernels, whole_dates(): pl.pallas_call(functools.partial(finish_body, bands), in_specs=[vmem], ou...  3.05 us
    broadcast_in_dim x1, local copies, waits for them, and re-layouts, whole_dates(): jnp.broadcast_to(clear_bits.reshape(1, blocks, 1, lanes), (strips, blocks...  1.32 us
    ppermute x1, starting transfers between devices, shifted(): lax.ppermute(value, axis, [(source, source + steps) for source in range(f...  1.29 us
    slice x1, local copies, waits for them, and re-layouts, whole_dates(): below = shifted(scenes[:, :, 0, :], 'band', -1)  1.22 us
  transfers between devices with their start and end apart: 2, of which 0 were waited for; matrix products, arithmetic and copies ran while one was open for 2% of the time, Pallas kernels for 11%

profile of v2, /device:TPU:0, one launch (start us, length us, event | category | flops | bytes accessed | tf_op | source)
XLA Modules:
  0.0 58.0 jit_solution(5219094760349310034)
XLA Ops:
  0.6 1.3 %broadcast_in_dim.8 = s32[32,4,1,128]{3,1,2,0:T(4,128)} broadcast(s32[4,128]{1,0:T(4,128)} %bitcast.13), dimensions={1,3} | broadcast | bytes 67584 | tf_op jit(solution)/shard_map/broadcast_in_dim | solution.py:706
  1.9 7.3 %all-to-all-start = ((s32[32,4,1,128]{3,1,2,0:T(4,128)}), s32[32,4,1,128]{3,1,2,0:T(4,128)S(1)}, u32[]{:S(2)}, u32[]{:S(2)}) async-start(s32[32,4,1,128]{3,1,2,0:T(4,128)} %broadcast_in_dim.8), calls=%async_computation | async-start | bytes 131072 | tf_op jit(solution)/shard_map/all_to_all | solution.py:707
  9.3 1.2 %slice.3 = bf16[60,6,1,128]{3,2,1,0:T(2,128)(2,1)S(1)} slice(bf16[60,6,32,128]{3,2,1,0:T(8,128)(2,1)} %scene_far.1), slice={[0:60], [0:6], [0:1], [0:128]} | slice | bytes 184320 | tf_op jit(solution)/shard_map/slice | solution.py:708
  10.5 1.3 %collective-permute-start = (bf16[60,6,128]{2,1,0:T(8,128)(2,1)S(1)}, bf16[60,6,128]{2,1,0:T(8,128)(2,1)S(1)}, u32[]{:S(2)}, u32[]{:S(2)}) collective-permute-start(bf16[60,6,128]{2,1,0:T(8,128)(2,1)S(1)} %bitcast.12), channel_id=1, source_target_pairs={{1,0},{2,1},{3,2},{4,3},{5,4},{6,5},{7,6},{8,7},{9,8},{10,9},{11,1... | collective-permute-start | bytes 276488 | tf_op jit(solution)/shard_map/ppermute | solution.py:23
  11.8 6.2 %resample.1 = (bf16[4,6,480,128]{3,2,1,0:T(8,128)(2,1)S(1)}, bf16[1408,512]{1,0:T(8,128)(2,1)}) custom-call(s32[2,60]{1,0:T(2,128)} %bitcast.14, s32[2,60]{1,0:T(2,128)} %bitcast.15, s32[1,60]{1,0:T(1,128)} %bitcast.16, bf16[256,512]{1,0:T(8,128)(2,1)} %constant.6.clone.smooth_far, bf16[60,6,32,128]{3,2,1,0:T(8,128)(2,1)} %scene_far.1), custom_call_target="tpu_custom_call" | custom-call | flops 20000000 | bytes 9000000 | tf_op jit(solution)/shard_map/resample/pallas_call | solution.py:721
  18.1 0.0 collective-permute-done.below_ref
  18.1 0.0 all-to-all-done
  18.1 4.1 %fit.1 = bf16[32,128,128]{2,1,0:T(8,128)(2,1)S(1)} custom-call(s32[1]{0:T(128)} %bitcast.place_ref, s32[128,128]{1,0:T(8,128)S(1)} %bitcast.11, bf16[60,6,128]{2,1,0:T(8,128)(2,1)S(1)} %collective-permute-done.below_ref, bf16[4,6,480,128]{3,2,1,0:T(8,128)(2,1)S(1)} %get-tuple-element.8.x_ref, bf16[1408,512]{1,0:T(8,128)(2,1)} %get-tuple-element.9.table_far), custom_call_target="tpu_custom_call" | custom-call | flops 20000000 | bytes 6000000 | tf_op jit(solution)/shard_map/fit/pallas_call | solution.py:746
  22.2 32.7 %all_to_all.10.recv_ref = bf16[32,128,128]{2,1,0:T(8,128)(2,1)S(1)} all-to-all(bf16[32,128,128]{2,1,0:T(8,128)(2,1)S(1)} %fit.1), channel_id=1, replica_groups=mesh['region'=1,'band'=32,'tile'=1,'sub'=1] {'band'}, dimensions={0} | all-to-all | bytes 2097152 | tf_op jit(solution)/shard_map/all_to_all | solution.py:769
  54.9 3.0 %finish.1 = (f32[48,4,1024]{2,1,0:T(4,128)}, f32[72,4,1024]{2,1,0:T(4,128)}, f32[6,4,1024]{2,1,0:T(4,128)}) custom-call(bf16[32,128,128]{2,1,0:T(8,128)(2,1)S(1)} %all_to_all.10.recv_ref), custom_call_target="tpu_custom_call" | custom-call | tf_op jit(solution)/shard_map/finish/pallas_call | solution.py:772
  (1 shorter events, 0.0 us)
Async XLA Ops:
  1.9 16.1 %all-to-all-start = ((s32[32,4,1,128]{3,1,2,0:T(4,128)}), s32[32,4,1,128]{3,1,2,0:T(4,128)S(1)}, u32[]{:S(2)}, u32[]{:S(2)}) async-start(s32[32,4,1,128]{3,1,2,0:T(4,128)} %broadcast_in_dim.8), calls=%async_computation | async-start | bytes 131072 | tf_op jit(solution)/shard_map/all_to_all | solution.py:707
  10.5 7.5 %collective-permute-start = (bf16[60,6,128]{2,1,0:T(8,128)(2,1)S(1)}, bf16[60,6,128]{2,1,0:T(8,128)(2,1)S(1)}, u32[]{:S(2)}, u32[]{:S(2)}) collective-permute-start(bf16[60,6,128]{2,1,0:T(8,128)(2,1)S(1)} %bitcast.12), channel_id=1, source_target_pairs={{1,0},{2,1},{3,2},{4,3},{5,4},{6,5},{7,6},{8,7},{9,8},{10,9},{11,1... | collective-permute-start | bytes 276488 | tf_op jit(solution)/shard_map/ppermute | solution.py:23
